TPU v7x, 32 devices: a whole 2x2x4 slice. The times are simulated.
32 devices in a mesh: row: 4 (over y, core), col: 8 (over z, x).
Axes of the slice: x: 2, y: 2, z: 4, core: 2. Of those that a mesh axis runs over, the one named last changes fastest.
Arguments:
- tokens: bfloat16 [256, 2, 4096], P(None, None, 'row'), may hold values from -6 to 6
- task_emb: bfloat16 [512, 1024], replicated, may hold values from -6 to 6
- gen_in: bfloat16 [1024, 512], replicated, may hold values from -0.1875 to 0.1875
- gen_a: bfloat16 [512, 4096, 16], P(None, ('row', 'col')), may hold values from -0.0078125 to 0.0078125
- gen_b: bfloat16 [512, 16, 14336], P(None, 'row', 'col'), may hold values from -0.125 to 0.125
- w_gate: bfloat16 [4096, 14336], P('row', 'col'), may hold values from -0.09375 to 0.09375
- w_up: bfloat16 [4096, 14336], P('row', 'col'), may hold values from -0.09375 to 0.09375
- w_down: bfloat16 [14336, 4096], P('col', 'row'), may hold values from -0.046875 to 0.046875
- group_count: int32 [64], replicated, may hold values from 1 to 16, 256 in all
- group_task: int32 [64], replicated, may hold values from 0 to 511, as said below
Outputs:
- mixed: bfloat16 [256, 2, 4096], P('col', None, 'row')
Inputs may be any that keep to these rules, and one draw needn't show every extreme that they name: `group_count`: requests in each group, in the order of the requests; they sum to 256 and the largest is 16. `group_task`: distinct task ids, one for each group.
All inputs are finite; a program needn't handle non-finite values.
Results may differ from a plain program's by a relative error of at most 0.0078.
Values may be sent and summed in bfloat16 or wider, within the bound.
A program may use at most 128 MiB of HBM per device.

v0:
```python
import jax
import jax.numpy as jnp
from jax import lax
from jax.sharding import PartitionSpec as P


def shards(tokens, task_emb, gen_in, gen_a, gen_b, w_gate, w_up, w_down, group_count, group_task):
    batch_size, draft_len, width_part = tokens.shape
    row_count = batch_size * draft_len
    flat_tokens = tokens.reshape(row_count, width_part)
    groups = group_count.shape[0]
    group_ends = jnp.cumsum(group_count)
    group_starts = group_ends - group_count
    request_ids = jnp.arange(batch_size, dtype=jnp.int32)
    membership = (request_ids[:, None] >= group_starts[None, :]) & (
        request_ids[:, None] < group_ends[None, :]
    )
    member_rows = jnp.repeat(membership, draft_len, axis=0)
    member_float = member_rows.astype(jnp.float32)
    member_half = member_rows.astype(jnp.bfloat16)
    chosen = jnp.take(task_emb, group_task, axis=0)
    hyper_out = jax.nn.silu(jnp.dot(chosen, gen_in, preferred_element_type=jnp.float32)).astype(
        jnp.bfloat16
    )
    hyper_width, slab_width, rank_dim = gen_a.shape
    a_local = jnp.dot(
        hyper_out,
        gen_a.reshape(hyper_width, slab_width * rank_dim),
        preferred_element_type=jnp.float32,
    )
    a_local = a_local.astype(jnp.bfloat16).reshape(groups, slab_width, rank_dim)
    a_local = a_local.transpose(1, 0, 2).reshape(slab_width, groups * rank_dim)
    wide_low = jnp.dot(
        flat_tokens,
        lax.all_gather(a_local, "col", axis=0, tiled=True),
        preferred_element_type=jnp.float32,
    )
    low_part = jnp.sum(
        wide_low.reshape(row_count, groups, rank_dim) * member_float[:, :, None], axis=1
    )
    gate_part = jnp.dot(flat_tokens, w_gate, preferred_element_type=jnp.float32)
    up_part = jnp.dot(flat_tokens, w_up, preferred_element_type=jnp.float32)
    _, rank_part, ff_part = gen_b.shape
    b_local = jnp.dot(
        hyper_out,
        gen_b.reshape(hyper_width, rank_part * ff_part),
        preferred_element_type=jnp.float32,
    )
    b_local = b_local.astype(jnp.bfloat16).reshape(groups, rank_part, ff_part)
    gate_total, up_total, low_sum = lax.psum((gate_part, up_part, low_part), "row")
    low_half = low_sum.astype(jnp.bfloat16)
    spread = member_half[:, :, None] * low_half[:, None, :]
    share_rows = spread.shape[0]
    block_piece = lax.all_gather(b_local, "row", axis=1, tiled=True)
    ranks_here = block_piece.shape[1]
    picked = spread.reshape(share_rows, groups * ranks_here)
    adapter_update = jnp.dot(
        picked,
        block_piece.reshape(groups * ranks_here, ff_part),
        preferred_element_type=jnp.float32,
    )
    hidden_state = (jax.nn.silu(gate_total) * (up_total + adapter_update)).astype(jnp.bfloat16)
    col_count = lax.axis_size("col")
    picked = hidden_state
    mixed = lax.psum_scatter(
        jnp.dot(picked, w_down, preferred_element_type=jnp.float32),
        "col",
        scatter_dimension=0,
        tiled=True,
    )
    return mixed.astype(jnp.bfloat16).reshape(batch_size // col_count, draft_len, w_down.shape[1])


def solution(mesh):
    in_specs = (
        P(None, None, "row"),
        P(),
        P(),
        P(None, ("row", "col"), None),
        P(None, "row", "col"),
        P("row", "col"),
        P("row", "col"),
        P("col", "row"),
        P(),
        P(),
    )
    out_specs = P("col", None, "row")
    return jax.shard_map(shards, mesh=mesh, in_specs=in_specs, out_specs=out_specs, check_vma=False)
```

profile of v0, /device:TPU:0, one launch (start us, length us, event | category | flops | bytes accessed | tf_op | source)
XLA Modules:
  0.0 278.1 jit_solution(9507470869285489578)
XLA Ops:
  7.4 0.7 compare_and_fusion
  8.1 0.7 compare_select_fusion
  8.8 3.9 %copy.28 = bf16[512,128,16]{0,2,1:T(8,128)(2,1)S(1)} copy(bf16[512,128,16]{1,2,0:T(8,128)(2,1)} %param.13) | data formatting | bytes 4194304 | tf_op args[3]
  12.7 0.7 gather_fusion
  13.4 1.6 multiply_convert_fusion
  15.0 0.7 convolution_convert_fusion.1
  15.8 0.3 copy.29
  16.1 1.3 copy.30
  17.4 0.0 all-reduce.3.cloned.1.call-start
  17.5 1.5 reshape.69
  18.9 6.2 %fusion.28 = f32[512,1792]{1,0:T(8,128)} fusion(bf16[512,1024]{1,0:T(8,128)(2,1)S(1)} %reshape.69, bf16[1024,1792]{1,0:T(8,128)(2,1)} %param.16), kind=kOutput, calls=%fused_computation.30 | convolution fusion | flops 1879048192 | bytes 8388608 | tf_op jit(solution)/shard_map/dot_general | solution.py:42
  25.1 3.9 %fusion.27 = f32[512,1792]{1,0:T(8,128)} fusion(bf16[512,1024]{1,0:T(8,128)(2,1)S(1)} %reshape.69, bf16[1024,1792]{1,0:T(8,128)(2,1)S(1)} %copy-done.2), kind=kOutput, calls=%fused_computation.29 | convolution fusion | flops 1879048192 | bytes 8388608 | tf_op jit(solution)/shard_map/dot_general | solution.py:41
  29.0 0.0 all-gather.5.cloned.1.call-start
  29.1 4.7 %copy.35 = bf16[64,8,4,1792]{3,1,2,0:T(8,128)(2,1)S(1)} copy(bf16[64,8,4,1792]{3,2,1,0:T(4,128)(2,1)} %bitcast.39) | data formatting | bytes 14680064
  33.8 1.4 convolution_convert_fusion
  35.2 1.0 copy.43
  36.2 0.1 copy.26
  36.3 0.1 reduce-window.8
  36.4 0.1 reduce
  36.6 0.1 broadcast_in_dim.24
  36.7 0.1 copy.27
  36.8 0.1 broadcast_in_dim.28
  36.9 0.1 copy.31
  37.0 33.6 %all-gather.3.cloned.1.call-done = bf16[1024,1024]{0,1:T(8,128)(2,1)} async-done(((bf16[128,1024]{0,1:T(8,128)(2,1)}), bf16[1024,1024]{0,1:T(8,128)(2,1)}) %all-gather.3.cloned.1.call-update) | async-done | bytes 2097168 | tf_op jit(solution)/shard_map/all_gather | solution.py:35
  70.6 2.9 %fusion.29 = f32[1024,512]{1,0:T(8,128)S(1)} fusion(bf16[1024,1024]{0,1:T(8,128)(2,1)} %all-gather.3.cloned.1.call-done, bf16[512,1024]{1,0:T(8,128)(2,1)S(1)} %reshape.69), kind=kOutput, calls=%fused_computation.31 | convolution fusion | flops 1073741824 | bytes 5242880 | tf_op jit(solution)/shard_map/dot_general | solution.py:33
  73.5 0.4 multiply_reduce_fusion
  73.9 12.4 %psum.23 = bf16[512,16]{0,1:T(8,128)(2,1)S(1)} all-reduce(f32[512,16]{0,1:T(8,128)S(1)} %multiply_reduce_fusion), channel_id=1, replica_groups=mesh['row'=4,'col'=8] {'row'}, use_global_device_ids=true, to_apply=%region_4.5 | all-reduce | flops 8192 | bytes 49152 | tf_op jit(solution)/shard_map/psum | solution.py:50
  86.3 102.3 %all-reduce.3.cloned.1.call-done = (f32[512,1792]{1,0:T(8,128)}, f32[512,1792]{1,0:T(8,128)}) async-done(((f32[512,1792]{1,0:T(8,128)}, f32[512,1792]{1,0:T(8,128)}), (f32[512,1792]{1,0:T(8,128)}, f32[512,1792]{1,0:T(8,128)})) %all-reduce.3.cloned.1.call-update) | async-done | bytes 7340048 | tf_op jit(solution)/shard_map/psum | solution.py:50
  188.6 12.0 %fusion.9 = f32[512,1024]{1,0:T(8,128)} fusion(bf16[1792,1024]{1,0:T(8,128)(2,1)} %param.17, f32[512,1792]{1,0:T(8,128)} %get-tuple-element.5, f32[512,1792]{1,0:T(8,128)} %get-tuple-element.6, bf16[64,16,1792]{2,0,1:T(8,128)(2,1)} %all-gather.5.cloned.1.call-done, bf16[512,16]{0,1:T(8,128)(2,1)S(1)} %psum.23, bf16[512,64]{0,1:T(8,128)(2,1)S(1)} %copy.27), kind=kOutput, calls=%fused_computation.11 | convolution fusion | flops 3765043200 | bytes 16859136 | tf_op jit(solution)/shard_map/dot_general | solution.py:66
  200.6 68.8 %reduce-scatter.2.cloned.1.call-done = f32[64,1024]{1,0:T(8,128)} async-done(((f32[512,1024]{1,0:T(8,128)}), f32[64,1024]{1,0:T(8,128)}) %reduce-scatter.2.cloned.1.call-update) | async-done | bytes 262160 | tf_op jit(solution)/shard_map/reduce_scatter | solution.py:65
  269.3 1.0 convert_element_type.49
  270.3 0.7 reshape.78
  (16 shorter events, 0.2 us)
Async XLA Ops:
  7.4 5.3 %copy-start = (bf16[512,1024]{1,0:T(8,128)(2,1)S(1)}, bf16[512,1024]{1,0:T(8,128)(2,1)}, u32[]{:S(2)}) copy-start(bf16[512,1024]{1,0:T(8,128)(2,1)} %param.11) | copy-start | bytes 3145732
  7.4 63.3 %all-gather.3.cloned.1.call-start = ((), (), s32[]{:S(2)}) async-start(), calls=%async_computation.1 | async-start | bytes 2359296 | tf_op jit(solution)/shard_map/all_gather | solution.py:35
  17.4 171.2 %all-reduce.3.cloned.1.call-start = ((), (), s32[]{:S(2)}) async-start(), calls=%async_computation.4 | async-start | bytes 14680064 | tf_op jit(solution)/shard_map/psum | solution.py:50
  18.9 6.2 %copy-start.2 = (bf16[1024,1792]{1,0:T(8,128)(2,1)S(1)}, bf16[1024,1792]{1,0:T(8,128)(2,1)}, u32[]{:S(2)}) copy-start(bf16[1024,1792]{1,0:T(8,128)(2,1)} %param.15) | copy-start | bytes 11010052
  29.0 159.6 %all-gather.5.cloned.1.call-start = ((), (), s32[]{:S(2)}) async-start(), calls=%async_computation.2 | async-start | bytes 4587520 | tf_op jit(solution)/shard_map/all_gather | solution.py:54
  33.8 2.5 copy-start.1
  36.2 233.2 %reduce-scatter.2.cloned.1.call-start = ((), (), s32[]{:S(2)}) async-start(), calls=%async_computation.3 | async-start | bytes 2359296 | tf_op jit(solution)/shard_map/reduce_scatter | solution.py:65
Sparse Core Ops, SparseCore 0:
  17.5 53.0 all-gather.2
  72.2 47.7 all-gather.4
  200.7 68.5 reduce-scatter.1
Sparse Core Ops, SparseCore 1:
  29.1 159.4 all-reduce.2
where the time goes:
time: 279 us; the launch traced here: 278 us
  waiting for transfers between devices  205 us (73%)
  matrix products  28.6 us (10%)
  between operations  14.7 us (5%)
  local copies, waits for them, and re-layouts  14.5 us (5%)
  blocking collectives  12.4 us (4%)
  other arithmetic  3.03 us (1%)
    psum x1, waiting for transfers between devices, shards(): lax.psum((gate_part, up_part, low_part), 'row')  102 us
    reduce_scatter x1, waiting for transfers between devices, shards(): lax.psum_scatter(jnp.dot(picked, w_down, preferred_element_type=jnp.float...  68.8 us
    all_gather x1, waiting for transfers between devices, shards(): lax.all_gather(a_local, 'col', axis=0, tiled=True)  33.6 us
    psum x1, blocking collectives, shards(): lax.psum((gate_part, up_part, low_part), 'row')  12.4 us
    dot_general x1, matrix products, shards(): jnp.dot(picked, w_down, preferred_element_type=jnp.float32)  12 us
    unnamed x8, local copies, waits for them, and re-layouts  8.6 us
    dot_general x1, matrix products, shards(): up_part = jnp.dot(flat_tokens, w_up, preferred_element_type=jnp.float32)  6.17 us
  transfers between devices with their start and end apart: 4, of which 3 were waited for; matrix products, arithmetic and copies ran while one was open for 8% of the time, Pallas kernels for 0%

commit v1 on v0

v1 whole, which is shorter than its diff:
```python
import jax
import jax.numpy as jnp
from jax import lax
from jax.sharding import PartitionSpec as P


def shards(tokens, task_emb, gen_in, gen_a, gen_b, w_gate, w_up, w_down, group_count, group_task):
    batch_size, draft_len, width_part = tokens.shape
    row_count = batch_size * draft_len
    flat_tokens = tokens.reshape(row_count, width_part)
    groups = group_count.shape[0]
    group_ends = jnp.cumsum(group_count)
    group_starts = group_ends - group_count
    request_ids = jnp.arange(row_count, dtype=jnp.int32) // draft_len
    member_rows = (request_ids[:, None] >= group_starts[None, :]) & (
        request_ids[:, None] < group_ends[None, :]
    )
    chosen = jnp.take(task_emb, group_task, axis=0)
    hyper_out = jax.nn.silu(jnp.dot(chosen, gen_in, preferred_element_type=jnp.float32)).astype(
        jnp.bfloat16
    )
    hyper_width, slab_width, rank_dim = gen_a.shape
    a_local = lax.dot_general(
        gen_a, hyper_out, (((0,), (1,)), ((), ())), preferred_element_type=jnp.float32
    ).astype(jnp.bfloat16)
    a_local = a_local.transpose(0, 1, 2).reshape(slab_width, rank_dim * groups)
    col = lax.axis_index("col")
    own = lax.dynamic_slice_in_dim(flat_tokens, col * slab_width, slab_width, axis=1)
    wide_low = jnp.dot(own, a_local, preferred_element_type=jnp.float32)
    low_part = jnp.sum(
        wide_low.reshape(row_count, rank_dim, groups)
        * member_rows.astype(jnp.float32)[:, None, :],
        axis=2,
    )
    low_half = lax.psum(low_part, ("row", "col")).astype(jnp.bfloat16)
    _, rank_part, ff_part = gen_b.shape
    row = lax.axis_index("row")
    low_own = lax.dynamic_slice_in_dim(low_half, row * rank_part, rank_part, axis=1)
    b_local = lax.dot_general(
        gen_b, hyper_out, (((0,), (1,)), ((), ())), preferred_element_type=jnp.float32
    ).astype(jnp.bfloat16)
    spread = jnp.where(member_rows[:, None, :], low_own[:, :, None], jnp.bfloat16(0))
    lora_part = lax.dot_general(
        spread, b_local, (((1, 2), (0, 2)), ((), ())), preferred_element_type=jnp.float32
    )
    gate_part = jnp.dot(flat_tokens, w_gate, preferred_element_type=jnp.float32)
    up_part = jnp.dot(flat_tokens, w_up, preferred_element_type=jnp.float32) + lora_part
    both = jnp.stack([gate_part, up_part]).astype(jnp.bfloat16)
    both = lax.psum_scatter(both, "row", scatter_dimension=1, tiled=True).astype(jnp.float32)
    hidden_own = (jax.nn.silu(both[0]) * both[1]).astype(jnp.bfloat16)
    hidden_state = lax.all_gather(hidden_own, "row", axis=0, tiled=True)
    mixed = lax.psum_scatter(
        jnp.dot(hidden_state, w_down, preferred_element_type=jnp.float32).astype(jnp.bfloat16),
        "col",
        scatter_dimension=0,
        tiled=True,
    )
    col_count = lax.axis_size("col")
    return mixed.reshape(batch_size // col_count, draft_len, w_down.shape[1])


def solution(mesh):
    in_specs = (
        P(None, None, "row"),
        P(),
        P(),
        P(None, ("row", "col"), None),
        P(None, "row", "col"),
        P("row", "col"),
        P("row", "col"),
        P("col", "row"),
        P(),
        P(),
    )
    out_specs = P("col", None, "row")
    return jax.shard_map(shards, mesh=mesh, in_specs=in_specs, out_specs=out_specs, check_vma=False)
```

time: 279 us -> 223 us (0.80)
  waiting for transfers between devices: 205 us -> 127 us
  blocking collectives: 12.4 us -> 42.1 us
  local copies, waits for them, and re-layouts: 14.5 us -> 6 us
  other arithmetic: 3.03 us -> 8.96 us
  matrix products: 28.6 us -> 24.9 us
    psum x1 -> x0, waiting for transfers between devices: 102 us -> none  [shards(): lax.psum((gate_part, up_part, low_part), 'row')]
    reduce_scatter x1 -> x2, waiting for transfers between devices: 68.8 us -> 106 us  [the longest x1 64.9 us: shards(): lax.psum_scatter(jnp.dot(hidden_state, w_down, preferred_element_type=jnp...]
    psum x1, blocking collectives: 12.4 us -> 42.1 us  [shards(): low_half = lax.psum(low_part, ('row', 'col')).astype(jnp.bfloat16)]
    all_gather x2 -> x1, waiting for transfers between devices: 33.6 us -> 21.2 us  [shards(): hidden_state = lax.all_gather(hidden_own, 'row', axis=0, tiled=True)]
    unnamed x8 -> x4, local copies, waits for them, and re-layouts: 8.6 us -> 0.01 us
    another operation x2 -> x3, other arithmetic: 0.2 us -> 4.39 us  [the longest x1 4.18 us: shards(): both = jnp.stack([gate_part, up_part]).astype(jnp.bfloat16)]
    dot_general x5 -> x4, matrix products: 23.2 us -> 19.9 us  [the longest x1 7.36 us: shards(): lax.dot_general(spread, b_local, (((1, 2), (0, 2)), ((), ())), preferred_...]
  transfers between devices with their start and end apart: 4 -> 3, of which waited for: 3 -> 3; matrix products, arithmetic and copies ran while one was open for 8% -> 0% of each run, Pallas kernels for 0% -> 0%
where the time goes in v1:
time: 223 us
  waiting for transfers between devices  127 us (57%)
  blocking collectives  42.1 us (19%)
  matrix products  24.9 us (11%)
  between operations  13.2 us (6%)
  other arithmetic  8.96 us (4%)
  local copies, waits for them, and re-layouts  6 us (3%)
    reduce_scatter x1, waiting for transfers between devices, shards(): lax.psum_scatter(jnp.dot(hidden_state, w_down, preferred_element_type=jnp...  64.9 us
    psum x1, blocking collectives, shards(): low_half = lax.psum(low_part, ('row', 'col')).astype(jnp.bfloat16)  42.1 us
    reduce_scatter x1, waiting for transfers between devices, shards(): lax.psum_scatter(both, 'row', scatter_dimension=1, tiled=True)  41.1 us
    all_gather x1, waiting for transfers between devices, shards(): hidden_state = lax.all_gather(hidden_own, 'row', axis=0, tiled=True)  21.2 us
    dot_general x1, matrix products, shards(): lax.dot_general(spread, b_local, (((1, 2), (0, 2)), ((), ())), preferred_...  7.36 us
    dot_general x1, matrix products, shards(): jnp.dot(flat_tokens, w_up, preferred_element_type=jnp.float32) + lora_part  6.05 us
    dot_general x1, matrix products, shards(): jnp.dot(hidden_state, w_down, preferred_element_type=jnp.float32)  5.64 us
  transfers between devices with their start and end apart: 3, of which 3 were waited for; matrix products, arithmetic and copies ran while one was open for 0% of the time, Pallas kernels for 0%

profile of v1, /device:TPU:0, one launch (start us, length us, event | category | flops | bytes accessed | tf_op | source)
XLA Modules:
  0.0 222.5 jit_solution(16900432833477011631)
XLA Ops:
  6.5 0.0 copy-start
  6.5 0.0 reduce-scatter.3.cloned.1.call-start
  6.5 0.8 compare_select_fusion
  7.3 0.7 compare_and_fusion.1
  8.0 0.7 copy.17
  8.8 0.1 reduce-window.8
  8.9 0.1 reduce
  9.0 0.7 sub.12
  9.6 1.5 reshape.147
  11.1 0.1 fusion.46
  11.2 2.2 gather_fusion
  13.4 1.6 fusion.34
  15.0 0.0 copy-done
  15.0 0.8 multiply_reduce_fusion
  15.8 42.1 %psum.7 = bf16[512,16]{0,1:T(8,128)(2,1)S(1)} all-reduce(f32[512,16]{0,1:T(8,128)S(1)} %multiply_reduce_fusion), channel_id=1, replica_groups=mesh['row'=4,'col'=8] {'row','col'}, use_global_device_ids=true, to_apply=%region_2.3 | all-reduce | flops 8192 | bytes 49152 | tf_op jit(solution)/shard_map/psum | solution.py:35
  58.0 0.0 copy-start.1
  58.0 6.0 %fusion.47 = f32[512,1792]{1,0:T(8,128)} fusion(bf16[512,1024]{1,0:T(8,128)(2,1)S(1)} %reshape.147, bf16[1024,1792]{1,0:T(8,128)(2,1)} %param.16), kind=kOutput, calls=%fused_computation.49 | convolution fusion | flops 1879048192 | bytes 8388608 | tf_op jit(solution)/shard_map/dot_general | solution.py:47
  64.0 3.4 %fusion.3 = bf16[1,512,1792]{2,1,0:T(8,128)(2,1)} fusion(bf16[512,1024]{1,0:T(8,128)(2,1)S(1)} %reshape.147, bf16[1024,1792]{1,0:T(8,128)(2,1)S(1)} %copy-done.1), kind=kOutput, calls=%fused_computation.7 | convolution fusion | flops 1879965696 | bytes 6553600 | tf_op jit(solution)/shard_map/dot_general | solution.py:46
  67.4 7.4 %fusion.4 = bf16[1,512,1792]{2,1,0:T(8,128)(2,1)} fusion(f32[512,1792]{1,0:T(8,128)} %fusion.47, bf16[64,512,1]{1,0,2:T(8,128)(2,1)S(1)} %fusion.34, bf16[512,4,1792]{2,1,0:T(4,128)(2,1)} %param.14, pred[512,64]{0,1:T(8,128)(4,1)S(1)} %get-tuple-element.6, bf16[512,4]{0,1:T(4,128)(2,1)S(1)} %dynamic-slice_convert_fusion), kind=kOutput, calls=%fused_computation.8 | convolution fusion | flops 941948928 | bytes 12947456 | tf_op jit(solution)/shard_map/dot_general | solution.py:43
  74.8 4.2 %pad_maximum_fusion = bf16[2,512,1792]{2,1,0:T(8,128)(2,1)} fusion(bf16[1,512,1792]{2,1,0:T(8,128)(2,1)} %fusion.4, bf16[1,512,1792]{2,1,0:T(8,128)(2,1)} %fusion.3), kind=kLoop, calls=%fused_computation.3 | loop fusion | flops 1835008 | bytes 7340032 | tf_op jit(solution)/shard_map/stack | solution.py:48
  79.0 0.0 reduce-scatter.3.cloned.1.call-update
  79.0 0.0 all-gather.2.cloned.1.call-start
  79.1 41.1 %reduce-scatter.3.cloned.1.call-done = bf16[2,128,1792]{2,1,0:T(8,128)(2,1)} async-done(((bf16[2,512,1792]{2,1,0:T(8,128)(2,1)}), bf16[2,128,1792]{2,1,0:T(8,128)(2,1)}) %reduce-scatter.3.cloned.1.call-update) | async-done | bytes 917520 | tf_op jit(solution)/shard_map/reduce_scatter | solution.py:49
  120.2 1.3 convert_element_type.42
  121.5 1.0 fusion.22
  122.5 0.0 all-gather.2.cloned.1.call-update
  122.5 0.0 reduce-scatter.5.cloned.1.call-start
  122.6 21.2 %all-gather.2.cloned.1.call-done = bf16[512,1792]{1,0:T(8,128)(2,1)} async-done(((bf16[128,1792]{1,0:T(8,128)(2,1)}), bf16[512,1792]{1,0:T(8,128)(2,1)}) %all-gather.2.cloned.1.call-update) | async-done | bytes 1835024 | tf_op jit(solution)/shard_map/all_gather | solution.py:51
  143.8 5.6 %convolution_convert_fusion.1 = bf16[512,1024]{1,0:T(8,128)(2,1)} fusion(bf16[512,1792]{1,0:T(8,128)(2,1)} %all-gather.2.cloned.1.call-done, bf16[1792,1024]{1,0:T(8,128)(2,1)} %param.17), kind=kOutput, calls=%fused_computation.14 | convolution fusion | flops 1879572480 | bytes 6553600 | tf_op jit(solution)/shard_map/dot_general | solution.py:53
  149.5 0.0 reduce-scatter.5.cloned.1.call-update
  149.5 64.9 %reduce-scatter.5.cloned.1.call-done = bf16[64,1024]{1,0:T(8,128)(2,1)} async-done(((bf16[512,1024]{1,0:T(8,128)(2,1)}), bf16[64,1024]{1,0:T(8,128)(2,1)}) %reduce-scatter.5.cloned.1.call-update) | async-done | bytes 131088 | tf_op jit(solution)/shard_map/reduce_scatter | solution.py:52
  214.4 1.6 reshape.151
  (4 shorter events, 0.0 us)
Async XLA Ops:
  6.5 8.5 %copy-start = (bf16[512,128,16]{1,2,0:T(8,128)(2,1)S(1)}, bf16[512,128,16]{1,2,0:T(8,128)(2,1)}, u32[]{:S(2)}) copy-start(bf16[512,128,16]{1,2,0:T(8,128)(2,1)} %param.13) | copy-start | bytes 6291460
  6.5 113.6 %reduce-scatter.3.cloned.1.call-start = ((), (), s32[]{:S(2)}) async-start(), calls=%async_computation.2 | async-start | bytes 4587520 | tf_op jit(solution)/shard_map/reduce_scatter | solution.py:49
  58.0 6.1 %copy-start.1 = (bf16[1024,1792]{1,0:T(8,128)(2,1)S(1)}, bf16[1024,1792]{1,0:T(8,128)(2,1)}, u32[]{:S(2)}) copy-start(bf16[1024,1792]{1,0:T(8,128)(2,1)} %param.15) | copy-start | bytes 11010052
  79.0 64.8 %all-gather.2.cloned.1.call-start = ((), (), s32[]{:S(2)}) async-start(), calls=%async_computation.3 | async-start | bytes 2293760 | tf_op jit(solution)/shard_map/all_gather | solution.py:51
  122.5 91.9 %reduce-scatter.5.cloned.1.call-start = ((), (), s32[]{:S(2)}) async-start(), calls=%async_computation.4 | async-start | bytes 1179648 | tf_op jit(solution)/shard_map/reduce_scatter | solution.py:52
Sparse Core Ops, SparseCore 0:
  79.1 41.0 reduce-scatter.2
  122.7 21.0 all-gather.1
  149.6 64.7 reduce-scatter.4

commit v2 on v1

v2 whole, which is shorter than its diff:
```python
import functools

import jax
import jax.numpy as jnp
from jax import lax
from jax.experimental import pallas as pl
from jax.experimental.pallas import tpu as pltpu
from jax.sharding import PartitionSpec as P

SUBROWS = 16


def tile_of(width):
    return 256 if width % 256 == 0 else 128


def layer_kernel(
    row_count, col_count, chunks,
    tok, spread, b_own, w_gate, w_up, w_down, out,
    part32, part16, pair_in, y_out, y_in, hid, mix32, mix16, x_in, z_out, z_in,
    pair_ss, pair_rs, y_ss, y_rs, ag_ss, ag_rs, fw_ss, fw_rs, x_ss, x_rs, z_ss, z_rs,
):
    row, col = lax.axis_index("row"), lax.axis_index("col")
    ys, zs = row_count // 2, col_count // 2
    y, core = row // 2, row % 2
    z, x = col // 2, col % 2
    rows = tok.shape[0] // chunks
    half = rows // 2
    piece = half // ys
    sub = half // zs
    ff = w_gate.shape[1]
    model = w_down.shape[1]

    row_pair = {"row": y * 2 + (1 - core)}
    col_pair = {"col": z * 2 + (1 - x)}
    y_peer = [{"row": ((y + q) % ys) * 2 + core} for q in range(1, ys)]
    z_peer = [{"col": ((z + q) % zs) * 2 + x} for q in range(1, zs)]

    barrier = pltpu.get_barrier_semaphore()
    everyone = [row_pair, col_pair] + y_peer + z_peer
    for peer in everyone:
        pl.semaphore_signal(
            barrier, inc=1, device_id=peer, device_id_type=pl.DeviceIdType.MESH
        )
    pl.semaphore_wait(barrier, len(everyone))

    sent = []

    def send(src, dst, ssem, rsem, peer):
        copy = pltpu.make_async_remote_copy(
            src_ref=src, dst_ref=dst, send_sem=ssem, recv_sem=rsem,
            device_id=peer, device_id_type=pl.DeviceIdType.MESH,
        )
        copy.start()
        sent.append(copy)
        return copy

    def at(start, size):
        return pl.ds(pl.multiple_of(start, SUBROWS), size)

    mine, other = at(core * half, half), at((1 - core) * half, half)
    own = at(core * half + y * piece, piece)
    x_mine, x_other = at(x * half, half), at((1 - x) * half, half)
    pair_c, y_c, ag_c, fw_c, x_c, z_c = {}, {}, {}, {}, {}, {}

    def gate_up(k):
        here = pl.ds(k * rows, rows)
        width = tile_of(ff)

        def body(n, carry):
            lo = pl.ds(pl.multiple_of(n * width, 128), width)
            hi = pl.ds(pl.multiple_of(ff + n * width, 128), width)
            gate = jnp.dot(tok[here, :], w_gate[:, lo], preferred_element_type=jnp.float32)
            up = jnp.dot(tok[here, :], w_up[:, lo], preferred_element_type=jnp.float32)
            up += jnp.dot(spread[here, :], b_own[:, lo], preferred_element_type=jnp.float32)
            part32[k, :, lo] = gate
            part32[k, :, hi] = up
            part16[k, :, lo] = gate.astype(jnp.bfloat16)
            part16[k, :, hi] = up.astype(jnp.bfloat16)
            return carry

        lax.fori_loop(0, ff // width, body, 0)
        pair_c[k] = send(part16.at[k, other], pair_in.at[k], pair_ss.at[k], pair_rs.at[k], row_pair)

    def add_pair(k):
        pair_c[k].wait_recv()
        total = part32[k, mine, :] + pair_in[k].astype(jnp.float32)
        part32[k, mine, :] = total
        y_out[k] = total.astype(jnp.bfloat16)
        y_c[k] = [
            send(
                y_out.at[k, at(((y + q) % ys) * piece, piece)], y_in.at[k, q - 1],
                y_ss.at[k, q - 1], y_rs.at[k, q - 1], y_peer[q - 1],
            )
            for q in range(1, ys)
        ]

    def activate(k):
        total = part32[k, own, :]
        for q in range(ys - 1):
            y_c[k][q].wait_recv()
            total += y_in[k, q].astype(jnp.float32)
        hid[k, own, :] = (jax.nn.silu(total[:, :ff]) * total[:, ff:]).astype(jnp.bfloat16)
        ag_c[k] = [
            send(hid.at[k, own], hid.at[k, own], ag_ss.at[k, q], ag_rs.at[k, q], y_peer[q])
            for q in range(ys - 1)
        ]

    def forward(k):
        for q in range(ys - 1):
            ag_c[k][q].wait_recv()
        fw_c[k] = send(hid.at[k, mine], hid.at[k, mine], fw_ss.at[k], fw_rs.at[k], row_pair)

    def down(k):
        fw_c[k].wait_recv()
        width = tile_of(model)

        def body(n, carry):
            lo = pl.ds(pl.multiple_of(n * width, 128), width)
            mix = jnp.dot(hid[k], w_down[:, lo], preferred_element_type=jnp.float32)
            mix32[k, :, lo] = mix
            mix16[k, :, lo] = mix.astype(jnp.bfloat16)
            return carry

        lax.fori_loop(0, model // width, body, 0)
        x_c[k] = send(mix16.at[k, x_other], x_in.at[k], x_ss.at[k], x_rs.at[k], col_pair)

    def add_x(k):
        x_c[k].wait_recv()
        total = mix32[k, x_mine, :] + x_in[k].astype(jnp.float32)
        mix32[k, x_mine, :] = total
        z_out[k] = total.astype(jnp.bfloat16)
        z_c[k] = [
            send(
                z_out.at[k, at(((z + q) % zs) * sub, sub)], z_in.at[k, q - 1],
                z_ss.at[k, q - 1], z_rs.at[k, q - 1], z_peer[q - 1],
            )
            for q in range(1, zs)
        ]

    def finish(k):
        total = mix32[k, at(x * half + z * sub, sub), :]
        for q in range(zs - 1):
            z_c[k][q].wait_recv()
            total += z_in[k, q].astype(jnp.float32)
        out[pl.ds(k * sub, sub), :] = total.astype(jnp.bfloat16)

    front = ((gate_up, 0), (add_pair, 1))
    middle = ((activate, 0),)
    back = ((forward, 0), (down, 1), (add_x, 2), (finish, 3))
    for stages in (front, middle, back):
        for step in range(chunks + stages[-1][1]):
            for stage, lag in stages:
                if 0 <= step - lag < chunks:
                    stage(step - lag)
    for copy in sent:
        copy.wait_send()


def shards(
    row_count, col_count,
    tokens, task_emb, gen_in, gen_a, gen_b, w_gate, w_up, w_down, group_count, group_task,
):
    batch_size, draft_len, width_part = tokens.shape
    total_rows = batch_size * draft_len
    groups = group_count.shape[0]
    chunks = total_rows // (col_count * SUBROWS)
    ys, zs = row_count // 2, col_count // 2

    def reorder(array):
        cut = array.reshape(zs, 2, chunks, SUBROWS, array.shape[-1])
        return cut.transpose(2, 1, 0, 3, 4).reshape(total_rows, array.shape[-1])

    flat_tokens = reorder(tokens)
    group_ends = jnp.cumsum(group_count)
    group_starts = group_ends - group_count
    request_ids = reorder(jnp.arange(total_rows, dtype=jnp.int32)[:, None] // draft_len)
    member_rows = (request_ids >= group_starts[None, :]) & (request_ids < group_ends[None, :])
    chosen = jnp.take(task_emb, group_task, axis=0)
    hyper_out = jax.nn.silu(jnp.dot(chosen, gen_in, preferred_element_type=jnp.float32)).astype(
        jnp.bfloat16
    )
    hyper_width, slab_width, rank_dim = gen_a.shape
    a_local = lax.dot_general(
        gen_a, hyper_out, (((0,), (1,)), ((), ())), preferred_element_type=jnp.float32
    ).astype(jnp.bfloat16)
    a_local = a_local.reshape(slab_width, rank_dim * groups)
    col, row = lax.axis_index("col"), lax.axis_index("row")
    own = lax.dynamic_slice_in_dim(flat_tokens, col * slab_width, slab_width, axis=1)
    wide_low = jnp.dot(own, a_local, preferred_element_type=jnp.float32)
    low_part = jnp.sum(
        wide_low.reshape(total_rows, rank_dim, groups)
        * member_rows.astype(jnp.float32)[:, None, :],
        axis=2,
    )
    low_half = lax.psum(low_part, ("row", "col")).astype(jnp.bfloat16)
    _, rank_part, ff = gen_b.shape
    low_own = lax.dynamic_slice_in_dim(low_half, row * rank_part, rank_part, axis=1)
    b_own = lax.dot_general(
        hyper_out, gen_b, (((1,), (0,)), ((), ())), preferred_element_type=jnp.float32
    ).astype(jnp.bfloat16)
    b_own = b_own.transpose(1, 0, 2).reshape(rank_part * groups, ff)
    spread = jnp.where(
        jnp.tile(member_rows, (1, rank_part)), jnp.repeat(low_own, groups, axis=1), jnp.bfloat16(0)
    )
    model = w_down.shape[1]
    rows = total_rows // chunks
    half = rows // 2
    bf, f32 = jnp.bfloat16, jnp.float32
    dma = pltpu.SemaphoreType.DMA
    y_sems, z_sems = max(ys - 1, 1), max(zs - 1, 1)
    vmem = pl.BlockSpec(memory_space=pltpu.VMEM)
    mixed = pl.pallas_call(
        functools.partial(layer_kernel, row_count, col_count, chunks),
        out_shape=jax.ShapeDtypeStruct((total_rows // col_count, model), bf),
        in_specs=[vmem] * 6,
        out_specs=vmem,
        scratch_shapes=[
            pltpu.VMEM((chunks, rows, 2 * ff), f32),
            pltpu.VMEM((chunks, rows, 2 * ff), bf),
            pltpu.VMEM((chunks, half, 2 * ff), bf),
            pltpu.VMEM((chunks, half, 2 * ff), bf),
            pltpu.VMEM((chunks, y_sems, half // ys, 2 * ff), bf),
            pltpu.VMEM((chunks, rows, ff), bf),
            pltpu.VMEM((chunks, rows, model), f32),
            pltpu.VMEM((chunks, rows, model), bf),
            pltpu.VMEM((chunks, half, model), bf),
            pltpu.VMEM((chunks, half, model), bf),
            pltpu.VMEM((chunks, z_sems, half // zs, model), bf),
            dma((chunks,)), dma((chunks,)),
            dma((chunks, y_sems)), dma((chunks, y_sems)),
            dma((chunks, y_sems)), dma((chunks, y_sems)),
            dma((chunks,)), dma((chunks,)),
            dma((chunks,)), dma((chunks,)),
            dma((chunks, z_sems)), dma((chunks, z_sems)),
        ],
        compiler_params=pltpu.CompilerParams(
            collective_id=0, has_side_effects=True, vmem_limit_bytes=60 * 1024 * 1024
        ),
        name="layer",
    )(flat_tokens, spread, b_own, w_gate, w_up, w_down)
    return mixed.reshape(batch_size // col_count, draft_len, model)


def solution(mesh):
    in_specs = (
        P(None, None, "row"),
        P(),
        P(),
        P(None, ("row", "col"), None),
        P(None, "row", "col"),
        P("row", "col"),
        P("row", "col"),
        P("col", "row"),
        P(),
        P(),
    )
    out_specs = P("col", None, "row")
    body = functools.partial(shards, mesh.shape["row"], mesh.shape["col"])
    return jax.shard_map(body, mesh=mesh, in_specs=in_specs, out_specs=out_specs, check_vma=False)
```

time: 223 us -> 123 us (0.55)
  waiting for transfers between devices: 127 us -> 0 us
  Pallas kernels: 0 us -> 61.5 us
  matrix products: 24.9 us -> 7.89 us
  between operations: 13.2 us -> 0.14 us
  other arithmetic: 8.96 us -> 1.04 us
  local copies, waits for them, and re-layouts: 6 us -> 9.53 us
    reduce_scatter x2 -> x0, waiting for transfers between devices: 106 us -> none  [the longest x1 64.9 us: shards(): lax.psum_scatter(jnp.dot(hidden_state, w_down, preferred_element_type=jnp...]
    pallas_call x0 -> x1, Pallas kernels: none -> 61.5 us  [shards(): pl.pallas_call(functools.partial(layer_kernel, row_count, col_count, chun...]
    all_gather x1 -> x0, waiting for transfers between devices: 21.2 us -> none  [shards(): hidden_state = lax.all_gather(hidden_own, 'row', axis=0, tiled=True)]
    dot_general x4 -> x1, matrix products: 22.4 us -> 5.46 us  [shards(): lax.dot_general(hyper_out, gen_b, (((1,), (0,)), ((), ())), preferred_ele...]
    another operation x3 -> x2, other arithmetic: 4.39 us -> 0.2 us  [the longest x1 4.18 us: shards(): both = jnp.stack([gate_part, up_part]).astype(jnp.bfloat16)]
    convert_element_type x2 -> x0, other arithmetic: 2.34 us -> none  [the longest x1 1.3 us: shards(): lax.psum_scatter(both, 'row', scatter_dimension=1, tiled=True)]
    reshape x2 -> x3, local copies, waits for them, and re-layouts: 3.07 us -> 5.18 us  [the longest x2 3.57 us: reorder(): cut = array.reshape(zs, 2, chunks, SUBROWS, array.shape[-1])]
  transfers between devices with their start and end apart: 3 -> 0, of which waited for: 3 -> 0; matrix products, arithmetic and copies ran while one was open for 0% -> 0% of each run, Pallas kernels for 0% -> 0%
where the time goes in v2:
time: 123 us; the launch traced here: 122 us
  Pallas kernels  61.5 us (50%)
  blocking collectives  42.1 us (34%)
  local copies, waits for them, and re-layouts  9.53 us (8%)
  matrix products  7.89 us (6%)
    pallas_call x1, Pallas kernels, shards(): pl.pallas_call(functools.partial(layer_kernel, row_count, col_count, chun...  61.5 us
    psum x1, blocking collectives, shards(): low_half = lax.psum(low_part, ('row', 'col')).astype(jnp.bfloat16)  42.1 us
    dot_general x1, matrix products, shards(): lax.dot_general(hyper_out, gen_b, (((1,), (0,)), ((), ())), preferred_ele...  5.46 us
    reshape x2, local copies, waits for them, and re-layouts, reorder(): cut = array.reshape(zs, 2, chunks, SUBROWS, array.shape[-1])  3.57 us
    gather x1, local copies, waits for them, and re-layouts, shards(): chosen = jnp.take(task_emb, group_task, axis=0)  2.51 us

profile of v2, /device:TPU:0, one launch (start us, length us, event | category | flops | bytes accessed | tf_op | source)
XLA Modules:
  0.0 122.2 jit_solution(9527517490028665425)
XLA Ops:
  0.0 0.0 copy-start
  0.0 0.9 copy.17
  0.9 0.1 reduce-window.8
  1.0 0.1 reduce
  1.1 0.7 sub.10
  1.8 0.1 ge.30
  1.9 0.1 fusion.31
  2.0 0.0 copy-start.2
  2.0 2.3 %reshape.272 = bf16[4,2,4,16,1024]{4,3,2,1,0:T(8,128)(2,1)} reshape(bf16[256,2,1024]{2,1,0:T(2,128)(2,1)} %param.10) | data formatting | bytes 2097152 | tf_op jit(solution)/shard_map/reshape | solution.py:171
  4.3 1.3 %copy.16 = bf16[4,2,4,16,1024]{4,3,0,1,2:T(8,128)(2,1)S(1)} copy(bf16[4,2,4,16,1024]{4,3,2,1,0:T(8,128)(2,1)} %reshape.272) | data formatting | bytes 2097152 | tf_op jit(solution)/shard_map/reshape | solution.py:171
  5.6 0.0 copy-start.1
  5.6 0.0 copy-done.2
  5.6 2.5 %gather_fusion = bf16[64,1024]{1,0:T(8,128)(2,1)S(1)} fusion(bf16[512,1024]{1,0:T(8,128)(2,1)} %param.11, s32[1024]{0:T(1024)S(1)} %pad_clamp_fusion), kind=kCustom, calls=%fused_computation | custom fusion | bytes 262400 | tf_op jit(solution)/shard_map/jit(_take)/gather | solution.py:179
  8.2 1.6 %fusion.20 = bf16[64,512,1]{1,0,2:T(8,128)(2,1)S(1)} fusion(bf16[1024,512]{1,0:T(8,128)(2,1)} %param.12, bf16[64,1024]{1,0:T(8,128)(2,1)S(1)} %gather_fusion, pred[64]{0:T(512)(128)(4,1)S(1)} %compare_and_fusion.1), kind=kOutput, calls=%fused_computation.14 | convolution fusion | flops 67338240 | bytes 1245248 | tf_op jit(solution)/shard_map/dot_general | solution.py:180
  9.8 0.0 copy-done
  9.8 0.8 multiply_reduce_fusion
  10.6 0.0 copy-done.1
  10.6 42.1 %psum.7 = bf16[512,16]{0,1:T(8,128)(2,1)S(1)} all-reduce(f32[512,16]{0,1:T(8,128)S(1)} %multiply_reduce_fusion), channel_id=1, replica_groups=mesh['row'=4,'col'=8] {'row','col'}, use_global_device_ids=true, to_apply=%region_2.3 | all-reduce | flops 8192 | bytes 49152 | tf_op jit(solution)/shard_map/psum | solution.py:196
  52.8 0.8 copy.20.spread
  53.6 5.5 %fusion.2 = bf16[64,4,1792]{2,0,1:T(8,128)(2,1)} fusion(bf16[64,512,1]{1,0,2:T(8,128)(2,1)S(1)} %fusion.20, bf16[512,4,1792]{2,1,0:T(4,128)(2,1)} %param.14), kind=kOutput, calls=%fused_computation.3 | convolution fusion | flops 470220800 | bytes 8323072 | tf_op jit(solution)/shard_map/dot_general | solution.py:199
  59.1 61.5 %layer.1 = bf16[64,1024]{1,0:T(8,128)(2,1)} custom-call(bf16[512,1024]{1,0:T(8,128)(2,1)} %bitcast.31, bf16[512,256]{1,0:T(8,128)(2,1)} %copy.20.spread, bf16[256,1792]{1,0:T(8,128)(2,1)} %bitcast.33, bf16[1024,1792]{1,0:T(8,128)(2,1)} %w_gate.1, bf16[1024,1792]{1,0:T(8,128)(2,1)} %w_up.1, bf16[1792,1024]{1,0:T(8,128)(2,1)} %w_down.1), custom_call_target="tpu_custom_call" | custom-call | tf_op jit(solution)/shard_map/layer/pallas_call | solution.py:213
  120.6 1.6 %reshape.278 = bf16[32,2,1024]{2,1,0:T(2,128)(2,1)} reshape(bf16[64,1024]{1,0:T(8,128)(2,1)} %layer.1) | data formatting | bytes 262144 | tf_op jit(solution)/shard_map/reshape | solution.py:242
  (6 shorter events, 0.1 us)
Async XLA Ops:
  0.0 9.8 %copy-start = (bf16[512,128,16]{1,2,0:T(8,128)(2,1)S(1)}, bf16[512,128,16]{1,2,0:T(8,128)(2,1)}, u32[]{:S(2)}) copy-start(bf16[512,128,16]{1,2,0:T(8,128)(2,1)} %param.13) | copy-start | bytes 6291460
  2.0 3.6 %copy-start.2 = (s32[64]{0:T(128)S(1)}, s32[64]{0:T(128)}, u32[]{:S(2)}) copy-start(s32[64]{0:T(128)} %param.19) | copy-start | bytes 772
  5.6 5.0 %copy-start.1 = (bf16[4,2,4,16,1024]{4,3,0,1,2:T(8,128)(2,1)}, bf16[4,2,4,16,1024]{4,3,0,1,2:T(8,128)(2,1)S(1)}, u32[]{:S(2)}) copy-start(bf16[4,2,4,16,1024]{4,3,0,1,2:T(8,128)(2,1)S(1)} %copy.16) | copy-start | bytes 3145732

commit v3 on v2

--- a/solution.py
+++ b/solution.py
@@ -16,9 +16,9 @@
 
 def layer_kernel(
     row_count, col_count, chunks,
-    tok, spread, b_own, w_gate, w_up, w_down, out,
-    part32, part16, pair_in, y_out, y_in, hid, mix32, mix16, x_in, z_out, z_in,
-    pair_ss, pair_rs, y_ss, y_rs, ag_ss, ag_rs, fw_ss, fw_rs, x_ss, x_rs, z_ss, z_rs,
+    tok, low_part, member, b_own, w_gate, w_up, w_down, out,
+    spread, low_in, low_row, low_all, part32, part16, pair_in, y_out, y_in, hid, mix32, mix16, x_in, z_out, z_in,
+    lr_ss, lr_rs, lc_ss, lc_rs, pair_ss, pair_rs, y_ss, y_rs, ag_ss, ag_rs, fw_ss, fw_rs, x_ss, x_rs, z_ss, z_rs,
 ):
     row, col = lax.axis_index("row"), lax.axis_index("col")
     ys, zs = row_count // 2, col_count // 2
@@ -37,7 +37,9 @@
     z_peer = [{"col": ((z + q) % zs) * 2 + x} for q in range(1, zs)]
 
     barrier = pltpu.get_barrier_semaphore()
-    everyone = [row_pair, col_pair] + y_peer + z_peer
+    row_peer = [{"row": (row + q) % row_count} for q in range(1, row_count)]
+    col_peer = [{"col": (col + q) % col_count} for q in range(1, col_count)]
+    everyone = row_peer + col_peer
     for peer in everyone:
         pl.semaphore_signal(
             barrier, inc=1, device_id=peer, device_id_type=pl.DeviceIdType.MESH
@@ -63,44 +65,76 @@
     x_mine, x_other = at(x * half, half), at((1 - x) * half, half)
     pair_c, y_c, ag_c, fw_c, x_c, z_c = {}, {}, {}, {}, {}, {}
 
-    def gate_up(k):
+    low_row_c = [
+        send(
+            low_part.at[(row + q) % row_count], low_in.at[q - 1],
+            lr_ss.at[q - 1], lr_rs.at[q - 1], row_peer[q - 1],
+        )
+        for q in range(1, row_count)
+    ]
+    low_col_c = []
+
+    def low_over_row():
+        total = low_part[row]
+        for q in range(row_count - 1):
+            low_row_c[q].wait_recv()
+            total += low_in[q]
+        low_row[...] = total
+        for q in range(col_count - 1):
+            low_col_c.append(
+                send(low_row, low_all.at[q], lc_ss.at[q], lc_rs.at[q], col_peer[q])
+            )
+
+    def low_over_col():
+        total = low_row[...]
+        for q in range(col_count - 1):
+            low_col_c[q].wait_recv()
+            total += low_all[q]
+        total = total.astype(jnp.bfloat16).astype(jnp.float32)
+        wide = [member[...] * total[r : r + 1, :] for r in range(total.shape[0])]
+        spread[...] = jnp.concatenate(wide, axis=0).T.astype(jnp.bfloat16)
+
+    def partial(k, which):
         here = pl.ds(k * rows, rows)
         width = tile_of(ff)
+        j = 2 * k + which
 
         def body(n, carry):
             lo = pl.ds(pl.multiple_of(n * width, 128), width)
-            hi = pl.ds(pl.multiple_of(ff + n * width, 128), width)
-            gate = jnp.dot(tok[here, :], w_gate[:, lo], preferred_element_type=jnp.float32)
-            up = jnp.dot(tok[here, :], w_up[:, lo], preferred_element_type=jnp.float32)
-            up += jnp.dot(spread[here, :], b_own[:, lo], preferred_element_type=jnp.float32)
-            part32[k, :, lo] = gate
-            part32[k, :, hi] = up
-            part16[k, :, lo] = gate.astype(jnp.bfloat16)
-            part16[k, :, hi] = up.astype(jnp.bfloat16)
+            weights = w_up if which else w_gate
+            part = jnp.dot(tok[here, :], weights[:, lo], preferred_element_type=jnp.float32)
+            if which:
+                part += jnp.dot(spread[here, :], b_own[:, lo], preferred_element_type=jnp.float32)
+            part32[j, :, lo] = part
+            part16[j, :, lo] = part.astype(jnp.bfloat16)
             return carry
 
         lax.fori_loop(0, ff // width, body, 0)
-        pair_c[k] = send(part16.at[k, other], pair_in.at[k], pair_ss.at[k], pair_rs.at[k], row_pair)
-
-    def add_pair(k):
-        pair_c[k].wait_recv()
-        total = part32[k, mine, :] + pair_in[k].astype(jnp.float32)
-        part32[k, mine, :] = total
-        y_out[k] = total.astype(jnp.bfloat16)
-        y_c[k] = [
+        pair_c[j] = send(part16.at[j, other], pair_in.at[j], pair_ss.at[j], pair_rs.at[j], row_pair)
+
+    def add_pair(j):
+        pair_c[j].wait_recv()
+        total = part32[j, mine, :] + pair_in[j].astype(jnp.float32)
+        part32[j, mine, :] = total
+        y_out[j] = total.astype(jnp.bfloat16)
+        y_c[j] = [
             send(
-                y_out.at[k, at(((y + q) % ys) * piece, piece)], y_in.at[k, q - 1],
-                y_ss.at[k, q - 1], y_rs.at[k, q - 1], y_peer[q - 1],
+                y_out.at[j, at(((y + q) % ys) * piece, piece)], y_in.at[j, q - 1],
+                y_ss.at[j, q - 1], y_rs.at[j, q - 1], y_peer[q - 1],
             )
             for q in range(1, ys)
         ]
 
+    def summed(j):
+        total = part32[j, own, :]
+        for q in range(ys - 1):
+            y_c[j][q].wait_recv()
+            total += y_in[j, q].astype(jnp.float32)
+        return total
+
     def activate(k):
-        total = part32[k, own, :]
-        for q in range(ys - 1):
-            y_c[k][q].wait_recv()
-            total += y_in[k, q].astype(jnp.float32)
-        hid[k, own, :] = (jax.nn.silu(total[:, :ff]) * total[:, ff:]).astype(jnp.bfloat16)
+        gate, up = summed(2 * k), summed(2 * k + 1)
+        hid[k, own, :] = (jax.nn.silu(gate) * up).astype(jnp.bfloat16)
         ag_c[k] = [
             send(hid.at[k, own], hid.at[k, own], ag_ss.at[k, q], ag_rs.at[k, q], y_peer[q])
             for q in range(ys - 1)
@@ -145,10 +179,20 @@
             total += z_in[k, q].astype(jnp.float32)
         out[pl.ds(k * sub, sub), :] = total.astype(jnp.bfloat16)
 
-    front = ((gate_up, 0), (add_pair, 1))
     middle = ((activate, 0),)
     back = ((forward, 0), (down, 1), (add_x, 2), (finish, 3))
-    for stages in (front, middle, back):
+    order = [(k, 0) for k in range(chunks)] + [(k, 1) for k in range(chunks)]
+    for i, (k, which) in enumerate(order):
+        if which and k == 0:
+            low_over_col()
+        partial(k, which)
+        if i == 0:
+            low_over_row()
+        else:
+            before = order[i - 1]
+            add_pair(2 * before[0] + before[1])
+    add_pair(2 * chunks - 1)
+    for stages in (middle, back):
         for step in range(chunks + stages[-1][1]):
             for stage, lag in stages:
                 if 0 <= step - lag < chunks:
@@ -181,28 +225,20 @@
         jnp.bfloat16
     )
     hyper_width, slab_width, rank_dim = gen_a.shape
-    a_local = lax.dot_general(
-        gen_a, hyper_out, (((0,), (1,)), ((), ())), preferred_element_type=jnp.float32
+    a_local = jnp.einsum(
+        "gh,hdr->grd", hyper_out, gen_a, preferred_element_type=jnp.float32
     ).astype(jnp.bfloat16)
-    a_local = a_local.reshape(slab_width, rank_dim * groups)
-    col, row = lax.axis_index("col"), lax.axis_index("row")
+    col = lax.axis_index("col")
     own = lax.dynamic_slice_in_dim(flat_tokens, col * slab_width, slab_width, axis=1)
-    wide_low = jnp.dot(own, a_local, preferred_element_type=jnp.float32)
-    low_part = jnp.sum(
-        wide_low.reshape(total_rows, rank_dim, groups)
-        * member_rows.astype(jnp.float32)[:, None, :],
-        axis=2,
-    )
-    low_half = lax.psum(low_part, ("row", "col")).astype(jnp.bfloat16)
+    wide_low = jnp.einsum("grd,td->grt", a_local, own, preferred_element_type=jnp.float32)
+    member = member_rows.T.astype(jnp.float32)
+    low_part = jnp.sum(wide_low * member[:, None, :], axis=0)
+    low_part = low_part.reshape(row_count, rank_dim // row_count, total_rows)
     _, rank_part, ff = gen_b.shape
-    low_own = lax.dynamic_slice_in_dim(low_half, row * rank_part, rank_part, axis=1)
     b_own = lax.dot_general(
         hyper_out, gen_b, (((1,), (0,)), ((), ())), preferred_element_type=jnp.float32
     ).astype(jnp.bfloat16)
     b_own = b_own.transpose(1, 0, 2).reshape(rank_part * groups, ff)
-    spread = jnp.where(
-        jnp.tile(member_rows, (1, rank_part)), jnp.repeat(low_own, groups, axis=1), jnp.bfloat16(0)
-    )
     model = w_down.shape[1]
     rows = total_rows // chunks
     half = rows // 2
@@ -213,22 +249,28 @@
     mixed = pl.pallas_call(
         functools.partial(layer_kernel, row_count, col_count, chunks),
         out_shape=jax.ShapeDtypeStruct((total_rows // col_count, model), bf),
-        in_specs=[vmem] * 6,
+        in_specs=[vmem] * 7,
         out_specs=vmem,
         scratch_shapes=[
-            pltpu.VMEM((chunks, rows, 2 * ff), f32),
-            pltpu.VMEM((chunks, rows, 2 * ff), bf),
-            pltpu.VMEM((chunks, half, 2 * ff), bf),
-            pltpu.VMEM((chunks, half, 2 * ff), bf),
-            pltpu.VMEM((chunks, y_sems, half // ys, 2 * ff), bf),
+            pltpu.VMEM((total_rows, rank_part * groups), bf),
+            pltpu.VMEM((row_count - 1, rank_part, total_rows), f32),
+            pltpu.VMEM((rank_part, total_rows), f32),
+            pltpu.VMEM((col_count - 1, rank_part, total_rows), f32),
+            pltpu.VMEM((2 * chunks, rows, ff), f32),
+            pltpu.VMEM((2 * chunks, rows, ff), bf),
+            pltpu.VMEM((2 * chunks, half, ff), bf),
+            pltpu.VMEM((2 * chunks, half, ff), bf),
+            pltpu.VMEM((2 * chunks, y_sems, half // ys, ff), bf),
             pltpu.VMEM((chunks, rows, ff), bf),
             pltpu.VMEM((chunks, rows, model), f32),
             pltpu.VMEM((chunks, rows, model), bf),
             pltpu.VMEM((chunks, half, model), bf),
             pltpu.VMEM((chunks, half, model), bf),
             pltpu.VMEM((chunks, z_sems, half // zs, model), bf),
-            dma((chunks,)), dma((chunks,)),
-            dma((chunks, y_sems)), dma((chunks, y_sems)),
+            dma((row_count - 1,)), dma((row_count - 1,)),
+            dma((col_count - 1,)), dma((col_count - 1,)),
+            dma((2 * chunks,)), dma((2 * chunks,)),
+            dma((2 * chunks, y_sems)), dma((2 * chunks, y_sems)),
             dma((chunks, y_sems)), dma((chunks, y_sems)),
             dma((chunks,)), dma((chunks,)),
             dma((chunks,)), dma((chunks,)),
@@ -238,7 +280,7 @@
             collective_id=0, has_side_effects=True, vmem_limit_bytes=60 * 1024 * 1024
         ),
         name="layer",
-    )(flat_tokens, spread, b_own, w_gate, w_up, w_down)
+    )(flat_tokens, low_part, member, b_own, w_gate, w_up, w_down)
     return mixed.reshape(batch_size // col_count, draft_len, model)
 
 

time: 123 us -> 82.8 us (0.67)
  blocking collectives: 42.1 us -> 0 us
  Pallas kernels: 61.5 us -> 63.9 us
    psum x1 -> x0, blocking collectives: 42.1 us -> none  [shards(): low_half = lax.psum(low_part, ('row', 'col')).astype(jnp.bfloat16)]
    pallas_call x1, Pallas kernels: 61.5 us -> 63.9 us  [shards(): pl.pallas_call(functools.partial(layer_kernel, row_count, col_count, chun...]
where the time goes in v3:
time: 82.8 us; the launch traced here: 82.5 us
  Pallas kernels  63.9 us (77%)
  local copies, waits for them, and re-layouts  9.35 us (11%)
  matrix products  8.04 us (10%)
  other arithmetic  1 us (1%)
    pallas_call x1, Pallas kernels, shards(): pl.pallas_call(functools.partial(layer_kernel, row_count, col_count, chun...  63.9 us
    dot_general x1, matrix products, shards(): lax.dot_general(hyper_out, gen_b, (((1,), (0,)), ((), ())), preferred_ele...  5.46 us
    reshape x2, local copies, waits for them, and re-layouts, reorder(): cut = array.reshape(zs, 2, chunks, SUBROWS, array.shape[-1])  3.61 us
    gather x1, local copies, waits for them, and re-layouts, shards(): chosen = jnp.take(task_emb, group_task, axis=0)  2.51 us

profile of v3, /device:TPU:0, one launch (start us, length us, event | category | flops | bytes accessed | tf_op | source)
XLA Modules:
  0.0 82.5 jit_solution(8491348887262266764)
XLA Ops:
  0.0 0.0 copy-start
  0.0 0.9 %copy.15 = s32[64,1]{1,0:T(8,128)S(1)} copy(s32[64,1]{0,1:T(1,128)} %bitcast.25) | data formatting | bytes 512 | tf_op jit(solution)/shard_map/reshape.188
  0.9 0.1 reduce-window.8
  1.0 0.1 reduce
  1.1 0.7 sub.10
  1.8 0.1 ge.28
  1.9 0.1 and_convert_fusion.member
  2.0 0.0 copy-start.2
  2.0 0.0 copy-start.3
  2.0 2.3 %reshape.206 = bf16[4,2,4,16,1024]{4,3,2,1,0:T(8,128)(2,1)} reshape(bf16[256,2,1024]{2,1,0:T(2,128)(2,1)} %param.10) | data formatting | bytes 2097152 | tf_op jit(solution)/shard_map/reshape | solution.py:215
  4.3 1.3 %copy.14 = bf16[4,2,4,16,1024]{4,3,0,1,2:T(8,128)(2,1)S(1)} copy(bf16[4,2,4,16,1024]{4,3,2,1,0:T(8,128)(2,1)} %reshape.206) | data formatting | bytes 2097152 | tf_op jit(solution)/shard_map/reshape | solution.py:215
  5.6 0.0 copy-start.1
  5.6 0.0 copy-done.3
  5.7 2.5 %gather_fusion = bf16[64,1024]{1,0:T(8,128)(2,1)S(1)} fusion(bf16[512,1024]{1,0:T(8,128)(2,1)} %param.11, s32[1024]{0:T(1024)S(1)} %pad_clamp_fusion), kind=kCustom, calls=%fused_computation | custom fusion | bytes 262400 | tf_op jit(solution)/shard_map/jit(_take)/gather | solution.py:223
  8.2 1.6 %fusion.15 = bf16[64,512,1]{1,0,2:T(8,128)(2,1)S(1)} fusion(bf16[1024,512]{1,0:T(8,128)(2,1)} %param.12, bf16[64,1024]{1,0:T(8,128)(2,1)S(1)} %gather_fusion, pred[64]{0:T(512)(128)(4,1)S(1)} %compare_and_fusion), kind=kOutput, calls=%fused_computation.14 | convolution fusion | flops 67338240 | bytes 1245248 | tf_op jit(solution)/shard_map/dot_general | solution.py:224
  9.8 0.0 copy-done
  9.8 0.5 fusion.5
  10.3 0.0 copy-done.2
  10.3 0.0 copy-done.1
  10.3 0.5 multiply_reduce_fusion
  10.8 0.6 reshape.210.low_part
  11.4 5.5 %fusion.2 = bf16[64,4,1792]{2,0,1:T(8,128)(2,1)} fusion(bf16[64,512,1]{1,0,2:T(8,128)(2,1)S(1)} %fusion.15, bf16[512,4,1792]{2,1,0:T(4,128)(2,1)} %param.14), kind=kOutput, calls=%fused_computation.3 | convolution fusion | flops 470220800 | bytes 8323072 | tf_op jit(solution)/shard_map/dot_general | solution.py:238
  16.9 63.9 %layer.1 = bf16[64,1024]{1,0:T(8,128)(2,1)} custom-call(bf16[512,1024]{1,0:T(8,128)(2,1)} %bitcast.23, f32[4,4,512]{2,1,0:T(4,128)} %reshape.210.low_part, f32[64,512]{1,0:T(8,128)} %copy-done.2, bf16[256,1792]{1,0:T(8,128)(2,1)} %bitcast.24, bf16[1024,1792]{1,0:T(8,128)(2,1)} %w_gate.1, bf16[1024,1792]{1,0:T(8,128)(2,1)} %w_up.1, bf16[1792,1024]{1,0:T(8,128)(2,1)} %w_down.1), custom_call_target="tpu_custom_call" | custom-call | tf_op jit(solution)/shard_map/layer/pallas_call | solution.py:249
  80.8 1.6 %reshape.212 = bf16[32,2,1024]{2,1,0:T(2,128)(2,1)} reshape(bf16[64,1024]{1,0:T(8,128)(2,1)} %layer.1) | data formatting | bytes 262144 | tf_op jit(solution)/shard_map/reshape | solution.py:284
  (4 shorter events, 0.0 us)
Async XLA Ops:
  0.0 9.8 %copy-start = (bf16[512,128,16]{1,2,0:T(8,128)(2,1)S(1)}, bf16[512,128,16]{1,2,0:T(8,128)(2,1)}, u32[]{:S(2)}) copy-start(bf16[512,128,16]{1,2,0:T(8,128)(2,1)} %param.13) | copy-start | bytes 6291460
  2.0 8.3 %copy-start.2 = (f32[64,512]{1,0:T(8,128)}, f32[64,512]{1,0:T(8,128)S(1)}, u32[]{:S(2)}) copy-start(f32[64,512]{1,0:T(8,128)S(1)} %and_convert_fusion.member) | copy-start | bytes 393220
  2.0 3.6 %copy-start.3 = (s32[64]{0:T(128)S(1)}, s32[64]{0:T(128)}, u32[]{:S(2)}) copy-start(s32[64]{0:T(128)} %param.19) | copy-start | bytes 772
  5.6 4.7 %copy-start.1 = (bf16[4,2,4,16,1024]{4,3,0,1,2:T(8,128)(2,1)}, bf16[4,2,4,16,1024]{4,3,0,1,2:T(8,128)(2,1)S(1)}, u32[]{:S(2)}) copy-start(bf16[4,2,4,16,1024]{4,3,0,1,2:T(8,128)(2,1)S(1)} %copy.14) | copy-start | bytes 3145732
